TPU v7x, 32 devices: a whole 2x2x4 slice. The times are simulated.
32 devices in a mesh: dp: 4 (over x, y), tp: 8 (over z, core).
Axes of the slice: x: 2, y: 2, z: 4, core: 2. Of those that a mesh axis runs over, the one named last changes fastest.
Arguments:
- x: bfloat16 [3072, 12288], P(('dp', 'tp')), parts along dimension 0
- w_gate: bfloat16 [12288, 33792], P(None, 'tp')
- w_up: bfloat16 [12288, 33792], P(None, 'tp')
- w_down: bfloat16 [33792, 12288], P('tp')
Outputs:
- output: bfloat16 [3072, 12288], P(('dp', 'tp')), parts along dimension 0
There are 4 independent parts. A program takes and returns all parts, laid end to end along the dimension named above; an argument that names none is the same for every part.
All inputs are finite; a program needn't handle non-finite values.
Results may differ from a plain program's by a relative error of at most 0.016.
Values are sent between devices in bfloat16 or wider.
A program may use at most 2 GiB of HBM per device.

v0:
```python
import jax
import jax.numpy as jnp
from jax import lax
from jax.sharding import PartitionSpec as P


def solution(mesh):
    def step(x, w_gate, w_up, w_down):
        rows = lax.all_gather(x, "tp", axis=0, tiled=True)
        gate = jnp.dot(rows, w_gate, preferred_element_type=jnp.float32)
        up = jnp.dot(rows, w_up, preferred_element_type=jnp.float32)
        hidden = (jax.nn.silu(gate) * up).astype(jnp.bfloat16)
        term = jnp.dot(hidden, w_down, preferred_element_type=jnp.float32).astype(jnp.bfloat16)
        return lax.psum_scatter(term, "tp", scatter_dimension=0, tiled=True)

    return jax.shard_map(
        step,
        mesh=mesh,
        in_specs=(P(("dp", "tp"), None), P(None, "tp"), P(None, "tp"), P("tp", None)),
        out_specs=P(("dp", "tp"), None),
        check_vma=False,
    )
```

profile of v0, /device:TPU:0, one launch (start us, length us, event | category | flops | bytes accessed | tf_op | source)
XLA Modules:
  0.0 652.9 jit_solution(2818454633415215523)
XLA Ops:
  6.5 0.0 all-gather.2.cloned.1.call-start
  6.5 0.7 all-gather.2.cloned.1.call-update
  7.3 0.0 reduce-scatter.2.cloned.1.call-start
  7.3 172.8 %all-gather.2.cloned.1.call-done = bf16[768,12288]{1,0:T(8,128)(2,1)} async-done(((bf16[96,12288]{1,0:T(8,128)(2,1)}), bf16[768,12288]{1,0:T(8,128)(2,1)}) %all-gather.2.cloned.1.call-update) | async-done | bytes 18874384 | tf_op jit(solution)/shard_map/all_gather | solution.py:9
  180.1 94.2 %fusion = f32[768,4224]{1,0:T(8,128)} fusion(bf16[768,12288]{1,0:T(8,128)(2,1)} %all-gather.2.cloned.1.call-done, bf16[12288,4224]{1,0:T(8,128)(2,1)} %param.5), kind=kOutput, calls=%fused_computation.2 | convolution fusion | flops 79725330432 | bytes 135659520 | tf_op jit(solution)/shard_map/dot_general | solution.py:10
  274.3 94.6 %multiply_convert_fusion = bf16[768,4224]{1,0:T(8,128)(2,1)S(1)} fusion(f32[768,4224]{1,0:T(8,128)} %fusion, bf16[768,12288]{1,0:T(8,128)(2,1)} %all-gather.2.cloned.1.call-done, bf16[12288,4224]{1,0:T(8,128)(2,1)} %param.6), kind=kOutput, calls=%fused_computation.1 | convolution fusion | flops 79744794624 | bytes 142147584 | tf_op jit(solution)/shard_map/dot_general | solution.py:11
  368.9 90.5 %convolution_convert_fusion = bf16[768,12288]{1,0:T(8,128)(2,1)} fusion(bf16[768,4224]{1,0:T(8,128)(2,1)S(1)} %multiply_convert_fusion, bf16[4224,12288]{1,0:T(8,128)(2,1)} %param.7), kind=kOutput, calls=%fused_computation | convolution fusion | flops 79734767616 | bytes 129171456 | tf_op jit(solution)/shard_map/dot_general | solution.py:13
  459.5 0.0 reduce-scatter.2.cloned.1.call-update
  459.5 186.6 %reduce-scatter.2.cloned.1.call-done = bf16[96,12288]{1,0:T(8,128)(2,1)} async-done(((bf16[768,12288]{1,0:T(8,128)(2,1)}), bf16[96,12288]{1,0:T(8,128)(2,1)}) %reduce-scatter.2.cloned.1.call-update) | async-done | bytes 2359312 | tf_op jit(solution)/shard_map/reduce_scatter | solution.py:14
Async XLA Ops:
  6.5 173.6 %all-gather.2.cloned.1.call-start = ((), (), s32[]{:S(2)}) async-start(), calls=%async_computation.1 | async-start | bytes 21233664 | tf_op jit(solution)/shard_map/all_gather | solution.py:9
  7.3 638.9 %reduce-scatter.2.cloned.1.call-start = ((), (), s32[]{:S(2)}) async-start(), calls=%async_computation.2 | async-start | bytes 21233664 | tf_op jit(solution)/shard_map/reduce_scatter | solution.py:14
Sparse Core Ops, SparseCore 0:
  9.0 171.0 all-gather.1
  459.6 186.4 reduce-scatter.1
where the time goes:
time: 653 us
  waiting for transfers between devices  360 us (55%)
  matrix products  279 us (43%)
  between operations  13.4 us (2%)
    reduce_scatter x1, waiting for transfers between devices, step(): return lax.psum_scatter(term, 'tp', scatter_dimension=0, tiled=True)  187 us
    all_gather x1, waiting for transfers between devices, step(): rows = lax.all_gather(x, 'tp', axis=0, tiled=True)  173 us
    dot_general x1, matrix products, step(): up = jnp.dot(rows, w_up, preferred_element_type=jnp.float32)  94.6 us
    dot_general x1, matrix products, step(): gate = jnp.dot(rows, w_gate, preferred_element_type=jnp.float32)  94.2 us
    dot_general x1, matrix products, step(): jnp.dot(hidden, w_down, preferred_element_type=jnp.float32)  90.5 us
  transfers between devices with their start and end apart: 2, of which 2 were waited for; matrix products, arithmetic and copies ran while one was open for 0% of the time, Pallas kernels for 0%

commit v1 on v0

v1 whole, which is shorter than its diff:
```python
import functools
import types

import jax
import jax.numpy as jnp
from jax import lax
from jax.experimental import pallas as pl
from jax.experimental.pallas import tpu as pltpu
from jax.sharding import PartitionSpec as P

BF, F32 = jnp.bfloat16, jnp.float32
LA, LR = 2, 3
RING = 4
SR = 3
A0 = 2


def config(rows_per_device, depth, hidden, rows, kc):
    c = types.SimpleNamespace()
    c.X, c.D, c.H = rows_per_device, depth, hidden
    c.KC, c.NK = kc, depth // kc
    c.NT = hidden // 128
    assert c.NT * 128 == hidden and c.NK * kc == depth
    c.UN = depth // 256
    c.NU = depth // 512
    c.rows = rows
    c.S = len(rows)
    c.off = [[sum(r[:i]) for i in range(5)] for r in rows]
    c.M = c.off[0][4]
    assert all(o[4] == c.M for o in c.off)
    c.RM = max(max(r) for r in rows)
    for z in range(4):
        assert sum(r[z] for r in rows) == c.X
    held = [[z for z in range(4) if r[z]] for r in rows]
    c.zmin, c.zmax = [h[0] for h in held], [h[-1] for h in held]
    c.ag_lag = [LA * max(max(z - c.zmin[s], c.zmax[s] - z) for z in range(4)) for s in range(c.S)]
    c.rs_lag = [A0 + LR * max(max(z, 3 - z) for z in held[s]) for s in range(c.S)]
    c.TA = [c.NK + lag + RING for lag in c.ag_lag]
    c.TR = [c.NU + lag + SR for lag in c.rs_lag]
    m = c.M
    c.scratch = [
        pltpu.VMEM((c.NK, 2 * m, kc), BF),
        pltpu.VMEM((c.NT, 2 * m, 256), F32),
        pltpu.VMEM((c.UN, m, 256), F32),
        pltpu.VMEM((2 * m, hidden), BF),
        pltpu.VMEM((2, kc, hidden), BF),
        pltpu.VMEM((2, kc, hidden), BF),
        pltpu.VMEM((4, hidden, 256), BF),
        pltpu.VMEM((SR, m, 512), BF),
        pltpu.VMEM((4, m, 512), BF),
        pltpu.VMEM((3, c.RM, 512), BF),
        pltpu.VMEM((2, SR, m, 512), BF),
        pltpu.VMEM((2, c.RM, 512), BF),
        pltpu.SemaphoreType.DMA((2, 2)),
        pltpu.SemaphoreType.DMA((4,)),
        pltpu.SemaphoreType.DMA,
        *[pltpu.SemaphoreType.DMA((3, c.NK)) for _ in rows],
        pltpu.SemaphoreType.DMA((3, RING)),
        *[pltpu.SemaphoreType.DMA((3, c.NU)) for _ in rows],
        pltpu.SemaphoreType.DMA((3, SR)),
        pltpu.SemaphoreType.DMA((7,)),
        pltpu.SemaphoreType.DMA((2,)),
        pltpu.SemaphoreType.REGULAR,
    ]
    return c


def kernel(c, x, wg, wu, wd, y, *refs):
    S, m = c.S, c.M
    land = [refs[3 * s : 3 * s + 3] for s in range(S)]
    refs = refs[3 * S :]
    (xs, acc, kept, hid, gw, uw, dw, ss, lin, fin, out, yst, gsem, dsem, xsem), refs = refs[:15], refs[15:]
    agr, ags, rsr = refs[:S], refs[S], refs[S + 1 : 2 * S + 1]
    rss, lsem, ysem, free = refs[2 * S + 1 :]

    tp = lax.axis_index("tp")
    z, core = tp // 2, lax.rem(tp, 2)
    sib = {"tp": z * 2 + 1 - core}

    def dev(zz):
        return {"tp": zz * 2 + core}

    def within(i, n):
        return jnp.logical_and(i >= 0, i < n)

    def repeat(lo, hi, f):
        lax.fori_loop(lo, hi, lambda t, _: (f(t), 0)[1], 0)

    def at_chip(f):
        for zz in range(4):
            pl.when(z == zz)(functools.partial(f, zz))

    def remote(src, dst, send, recv, to):
        return pltpu.make_async_remote_copy(
            src_ref=src, dst_ref=dst, send_sem=send, recv_sem=recv,
            device_id=to, device_id_type=pl.DeviceIdType.MESH,
        )

    def gcopies(k, slot):
        at = pl.ds(pl.multiple_of(k * c.KC, c.KC), c.KC)
        return [
            pltpu.make_async_copy(wg.at[at, :], gw.at[slot], gsem.at[0, slot]),
            pltpu.make_async_copy(wu.at[at, :], uw.at[slot], gsem.at[1, slot]),
        ]

    def dcopy(n, slot):
        at = pl.ds(pl.multiple_of(n * 256, 256), 256)
        return pltpu.make_async_copy(wd.at[:, at], dw.at[slot], dsem.at[slot])

    def ag_rows(s, zz, way):
        o = c.off[s]
        return [(0, o[min(zz + 1, 4)]), (o[zz], m), (0, m)][way]

    def ag_copy(s, zz, way, j):
        a, b = ag_rows(s, zz, way)
        to = [lambda: dev(zz + 1), lambda: dev(zz - 1), lambda: sib][way]()
        dst = pl.ds(m, m) if way == 2 else pl.ds(a, b - a)
        return remote(
            xs.at[j, pl.ds(a, b - a), :], xs.at[j, dst, :],
            ags.at[way, lax.rem(j + 2 * RING, RING)], agr[s].at[way, j], to,
        )

    def ag_tick(s, tau):
        def at(zz):
            up, down = zz - c.zmin[s], c.zmax[s] - zz
            lags = [max(up, 0), max(down, 0), max(up, down)]
            for way in range(3):
                j = tau - LA * lags[way]
                a, b = ag_rows(s, zz, way)
                sends = b > a and (way == 2 or (zz < 3 if way == 0 else zz > 0))
                before = zz - 1 if way == 0 else zz + 1
                takes = way < 2 and 0 <= before < 4
                if takes:
                    a, b = ag_rows(s, before, way)
                    takes = b > a

                def take(j=j, way=way, before=before):
                    ag_copy(s, before, way, j).wait_recv()

                def sent(j=j, way=way):
                    ag_copy(s, zz, way, j - RING).wait_send()

                def send(j=j, way=way):
                    ag_copy(s, zz, way, j).start()

                if takes:
                    pl.when(within(j, c.NK))(take)
                if sends:
                    pl.when(within(j - RING, c.NK))(sent)
                    pl.when(within(j, c.NK))(send)

        at_chip(at)

    def rs_rows(s, zz, way):
        o = c.off[s]
        return [(o[min(zz + 1, 4)], m), (0, o[zz]), (0, m)][way]

    def rs_copy(s, zz, way, u):
        a, b = rs_rows(s, zz, way)
        rows = pl.ds(a, b - a)
        slot = lax.rem(u + 2 * SR, SR)
        to = [lambda: dev(zz + 1), lambda: dev(zz - 1), lambda: sib][way]()
        src = ss.at[slot, rows, :] if way == 2 else out.at[way, slot, rows, :]
        return remote(src, land[s][way].at[u, rows, :], rss.at[way, slot], rsr[s].at[way, u], to)

    def rs_takes(s, zz, way):
        before = zz - 1 if way == 0 else zz + 1
        if not 0 <= before < 4:
            return False
        a, b = rs_rows(s, before, way)
        return b > a

    def rs_sends(s, zz, way):
        a, b = rs_rows(s, zz, way)
        return b > a and (zz < 3 if way == 0 else zz > 0)

    def rs_unit(s, zz, part, tau):
        return tau - A0 - LR * [zz, 3 - zz, max(zz, 3 - zz)][part]

    def rs_loads(s, zz, part, u):
        sb = land[s][2]
        if part == 2:
            rows, n = pl.ds(c.off[s][zz], c.rows[s][zz]), pl.ds(0, c.rows[s][zz])
            cps = [(sb.at[u, rows, :], fin.at[2, n, :], 6)]
            for way in range(2):
                if rs_takes(s, zz, way):
                    cps.append((land[s][way].at[u, rows, :], fin.at[way, n, :], 4 + way))
        else:
            a, b = rs_rows(s, zz, part)
            rows = pl.ds(a, b - a)
            cps = [(sb.at[u, rows, :], lin.at[2 + part, rows, :], 2 + part)]
            if rs_takes(s, zz, part):
                cps.append((land[s][part].at[u, rows, :], lin.at[part, rows, :], part))
        return [pltpu.make_async_copy(p, q, lsem.at[i]) for p, q, i in cps]

    def rs_parts(s, zz):
        return [p for p in range(3) if (c.rows[s][zz] > 0 if p == 2 else rs_sends(s, zz, p))]

    def rs_first(s, tau):
        @pl.when(within(tau - A0, c.NU))
        def _():
            rs_copy(s, 0, 2, tau - A0).wait_recv()

        def at(zz):
            for way in range(2):
                if rs_takes(s, zz, way):
                    u = rs_unit(s, zz, way, tau)

                    @pl.when(within(u, c.NU))
                    def _(u=u, way=way):
                        rs_copy(s, zz - 1 if way == 0 else zz + 1, way, u).wait_recv()

            for part in rs_parts(s, zz):
                u = rs_unit(s, zz, part, tau)

                @pl.when(within(u, c.NU))
                def _(u=u, part=part):
                    for cp in rs_loads(s, zz, part, u):
                        cp.start()

        at_chip(at)

    def rs_second(s, tau):
        def at(zz):
            for part in rs_parts(s, zz):
                u = rs_unit(s, zz, part, tau)
                if part == 2:
                    a, b = c.off[s][zz], c.off[s][zz + 1]
                    ins, to = (fin.at[2], fin.at[0], fin.at[1]), yst.at[lax.rem(u + 4, 2)]
                    takes, lo, n = [rs_takes(s, zz, 0), rs_takes(s, zz, 1)], a, 2
                else:
                    a, b = rs_rows(s, zz, part)
                    ins, to = (lin.at[2 + part], lin.at[part]), out.at[part, lax.rem(u + 2 * SR, SR)]
                    takes, lo, n = [rs_takes(s, zz, part)], 0, SR

                @pl.when(within(u - n, c.NU))
                def _(u=u, part=part):
                    if part == 2:
                        ystore(s, zz, u - 2).wait()
                    else:
                        rs_copy(s, zz, part, u - SR).wait_send()

                @pl.when(within(u, c.NU))
                def _(u=u, part=part, a=a, b=b, ins=ins, to=to, takes=takes, lo=lo):
                    for cp in rs_loads(s, zz, part, u):
                        cp.wait()
                    rows = pl.ds(a - lo, b - a)
                    for h in range(2):
                        cols = pl.ds(256 * h, 256)
                        v = kept[2 * u + h, pl.ds(a, b - a), :] + ins[0][rows, cols].astype(F32)
                        for i, take in enumerate(takes):
                            if take:
                                v = v + ins[1 + i][rows, cols].astype(F32)
                        to[rows, cols] = v.astype(BF)

            for part in rs_parts(s, zz):
                u = rs_unit(s, zz, part, tau)

                @pl.when(within(u, c.NU))
                def _(u=u, part=part):
                    if part == 2:
                        ystore(s, zz, u).start()
                    else:
                        rs_copy(s, zz, part, u).start()

        at_chip(at)

    def ystore(s, zz, u):
        r, r0 = c.rows[s][zz], sum(c.rows[t][zz] for t in range(s))
        slot = lax.rem(u + 4, 2)
        at = (pl.ds(r0, r), pl.ds(pl.multiple_of(u * 512, 512), 512))
        return pltpu.make_async_copy(yst.at[slot, pl.ds(0, r), :], y.at[at], ysem.at[slot])

    def gate_up(s, before, after):
        def chunk(k):
            slot = lax.rem(k, 2)
            for cp in gcopies(k, slot):
                cp.wait()
            ag_copy(s, 0, 2, k).wait_recv()
            if s + 1 < S:
                for cp in gcopies(lax.rem(k + 1, c.NK), 1 - slot):
                    cp.start()
            else:

                @pl.when(k + 1 < c.NK)
                def _():
                    for cp in gcopies(k + 1, 1 - slot):
                        cp.start()

            before(k)
            for t in range(c.NT):
                cols = pl.ds(t * 128, 128)
                w = jnp.concatenate([gw[slot, :, cols], uw[slot, :, cols]], axis=1)
                acc[t] += jnp.dot(xs[k], w, preferred_element_type=F32)
            after(k)

        repeat(0, c.NK, chunk)

    def activate():
        def act(t):
            g, u = acc[t, :, pl.ds(0, 128)], acc[t, :, pl.ds(128, 128)]
            h = (g * jax.nn.sigmoid(g)) * u
            hid[:, pl.ds(pl.multiple_of(t * 128, 128), 128)] = h.astype(BF)
            acc[t] = jnp.zeros((2 * m, 256), F32)

        repeat(0, c.NT, act)

    def down(s, before, after):
        def unit(u):
            half = 2 * lax.rem(u, 2)
            for h in range(2):
                dcopy(0, half + h).wait()
            for h in range(2):
                if s + 1 < S:
                    dcopy(lax.rem(2 * u + 2 + h, c.UN), 2 - half + h).start()
                else:

                    @pl.when(u + 1 < c.NU)
                    def _(h=h):
                        dcopy(2 * u + 2 + h, 2 - half + h).start()

            @pl.when(u >= SR)
            def _():
                rs_copy(s, 0, 2, u - SR).wait_send()

            before(u)
            slot = lax.rem(u, SR)
            for h in range(2):
                v = jnp.dot(hid[...], dw[half + h], preferred_element_type=F32)
                kept[2 * u + h] = v[:m]
                ss[slot, :, pl.ds(256 * h, 256)] = v[m:].astype(BF)
            rs_copy(s, 0, 2, u).start()
            after(u)

        repeat(0, c.NU, unit)
        for i in range(SR):
            rs_copy(s, 0, 2, c.NU - SR + i).wait_send()

    def own(s, zz, j):
        r0 = sum(c.rows[t][zz] for t in range(s))
        at = (pl.ds(r0, c.rows[s][zz]), pl.ds(pl.multiple_of(j * c.KC, c.KC), c.KC))
        return pltpu.make_async_copy(x.at[at], xs.at[j, pl.ds(c.off[s][zz], c.rows[s][zz]), :], xsem)

    def own_start(s):
        def at(zz):
            if c.rows[s][zz]:
                repeat(0, c.NK, lambda j: own(s, zz, j).start())

        at_chip(at)

    def own_wait(s):
        def at(zz):
            if c.rows[s][zz]:
                part = xs.at[:, pl.ds(c.off[s][zz], c.rows[s][zz]), :]
                pltpu.make_async_copy(part, part, xsem).wait()

        at_chip(at)

    def tell(sem):
        def signal(to):
            pl.semaphore_signal(sem, inc=1, device_id=to, device_id_type=pl.DeviceIdType.MESH)

        signal(sib)
        pl.when(z < 3)(lambda: signal(dev(z + 1)))
        pl.when(z > 0)(lambda: signal(dev(z - 1)))

    def hear(sem):
        pl.semaphore_wait(sem, 1 + (z < 3).astype(jnp.int32) + (z > 0).astype(jnp.int32))

    tell(pltpu.get_barrier_semaphore())
    own_start(0)
    for cp in gcopies(0, 0):
        cp.start()
    for n in range(2):
        dcopy(n, n).start()

    def clear(t):
        acc[t] = jnp.zeros((2 * m, 256), F32)

    own_wait(0)
    hear(pltpu.get_barrier_semaphore())
    na, nd = c.ag_lag[0] + 2, c.NU // 2
    repeat(0, 2, lambda t: ag_tick(0, t))
    repeat(0, c.NT, clear)
    repeat(2, na, lambda t: ag_tick(0, t))
    nothing = lambda t: None
    gate_up(0, nothing, lambda k: ag_tick(0, k + na))
    repeat(c.NK + na, c.TA[0], lambda t: ag_tick(0, t))
    tell(free)
    own_start(1)
    activate()

    def before(u):
        @pl.when(u == 0)
        def _():
            own_wait(1)
            hear(free)

        pl.when(lax.rem(u, 2) == 0)(lambda: ag_tick(1, u // 2))
        pl.when(lax.rem(u, 2) == 1)(lambda: rs_first(0, u // 2))

    down(0, before, lambda u: pl.when(lax.rem(u, 2) == 1)(lambda: rs_second(0, u // 2)))

    def after(k):
        rs_second(0, k + nd)
        ag_tick(1, k + nd)

    gate_up(1, lambda k: rs_first(0, k + nd), after)

    def both(s):
        def run(t):
            rs_first(s, t)
            rs_second(s, t)
        return run

    repeat(c.NK + nd, max(c.TA[1], c.NK + nd), lambda t: ag_tick(1, t))
    repeat(c.NK + nd, max(c.TR[0], c.NK + nd), both(0))
    activate()
    down(1, lambda u: rs_first(1, u), lambda u: rs_second(1, u))
    repeat(c.NU, c.TR[1], both(1))


def block(c, x, wg, wu, wd):
    lands = [jax.ShapeDtypeStruct((c.NU, c.M, 512), BF) for _ in range(3 * c.S)]
    hbm = pl.BlockSpec(memory_space=pltpu.HBM)
    outs = pl.pallas_call(
        functools.partial(kernel, c),
        out_shape=[jax.ShapeDtypeStruct((c.X, c.D), BF), *lands],
        in_specs=[hbm] * 4,
        out_specs=[hbm] * (1 + len(lands)),
        scratch_shapes=c.scratch,
        compiler_params=pltpu.CompilerParams(
            collective_id=0, has_side_effects=True, vmem_limit_bytes=67043328
        ),
        name="mlp",
    )(x, wg, wu, wd)
    return outs[0]


ROWS = [[32,64,64,32],[64,32,32,64]]


def solution(mesh):
    def step(x, w_gate, w_up, w_down):
        c = config(x.shape[0], x.shape[1], w_gate.shape[1], ROWS, 512)
        return block(c, x, w_gate, w_up, w_down)

    return jax.shard_map(
        step,
        mesh=mesh,
        in_specs=(P(("dp", "tp"), None), P(None, "tp"), P(None, "tp"), P("tp", None)),
        out_specs=P(("dp", "tp"), None),
        check_vma=False,
    )
```

time: 653 us -> 367 us (0.56)
  Pallas kernels: 0 us -> 362 us
  waiting for transfers between devices: 360 us -> 0 us
  matrix products: 279 us -> 0 us
  between operations: 13.4 us -> 0.01 us
    pallas_call x0 -> x1, Pallas kernels: none -> 362 us  [block(): pl.pallas_call(functools.partial(kernel, c), out_shape=[jax.ShapeDtypeStr...]
    dot_general x3 -> x0, matrix products: 279 us -> none  [the longest x1 94.6 us: step(): up = jnp.dot(rows, w_up, preferred_element_type=jnp.float32)]
    reduce_scatter x1 -> x0, waiting for transfers between devices: 187 us -> none  [step(): return lax.psum_scatter(term, 'tp', scatter_dimension=0, tiled=True)]
    all_gather x1 -> x0, waiting for transfers between devices: 173 us -> none  [step(): rows = lax.all_gather(x, 'tp', axis=0, tiled=True)]
  transfers between devices with their start and end apart: 2 -> 0, of which waited for: 2 -> 0; matrix products, arithmetic and copies ran while one was open for 0% -> 0% of each run, Pallas kernels for 0% -> 0%
where the time goes in v1:
time: 367 us; the launch traced here: 365 us
  Pallas kernels  362 us (99%)
    pallas_call x1, Pallas kernels, block(): pl.pallas_call(functools.partial(kernel, c), out_shape=[jax.ShapeDtypeStr...  362 us

profile of v1, /device:TPU:0, one launch (start us, length us, event | category | flops | bytes accessed | tf_op | source)
XLA Modules:
  0.0 364.9 jit_solution(15166346102728429498)
XLA Ops:
  0.0 361.7 %mlp.1 = (bf16[96,12288]{1,0:T(8,128)(2,1)}, bf16[24,192,512]{2,1,0:T(8,128)(2,1)}, bf16[24,192,512]{2,1,0:T(8,128)(2,1)}, bf16[24,192,512]{2,1,0:T(8,128)(2,1)}...) custom-call(bf16[96,12288]{1,0:T(8,128)(2,1)} %x.1, ...), custom_call_target="tpu_custom_call" | custom-call | tf_op jit(solution)/shard_map/mlp/pallas_call | solution.py:426
  361.7 3.2 copy.6

commit v2 on v1

--- a/solution.py
+++ b/solution.py
@@ -9,10 +9,11 @@
 from jax.sharding import PartitionSpec as P
 
 BF, F32 = jnp.bfloat16, jnp.float32
-LA, LR = 2, 3
+LA = 2
+LR = (2, 2)
 RING = 4
 SR = 3
-A0 = 2
+A0 = (0, 1)
 
 
 def config(rows_per_device, depth, hidden, rows, kc):
@@ -34,7 +35,7 @@
     held = [[z for z in range(4) if r[z]] for r in rows]
     c.zmin, c.zmax = [h[0] for h in held], [h[-1] for h in held]
     c.ag_lag = [LA * max(max(z - c.zmin[s], c.zmax[s] - z) for z in range(4)) for s in range(c.S)]
-    c.rs_lag = [A0 + LR * max(max(z, 3 - z) for z in held[s]) for s in range(c.S)]
+    c.rs_lag = [A0[s] + LR[s] * max(max(z, 3 - z) for z in held[s]) for s in range(c.S)]
     c.TA = [c.NK + lag + RING for lag in c.ag_lag]
     c.TR = [c.NU + lag + SR for lag in c.rs_lag]
     m = c.M
@@ -45,14 +46,14 @@
         pltpu.VMEM((2 * m, hidden), BF),
         pltpu.VMEM((2, kc, hidden), BF),
         pltpu.VMEM((2, kc, hidden), BF),
-        pltpu.VMEM((4, hidden, 256), BF),
+        pltpu.VMEM((5, hidden, 256), BF),
         pltpu.VMEM((SR, m, 512), BF),
         pltpu.VMEM((4, m, 512), BF),
         pltpu.VMEM((3, c.RM, 512), BF),
         pltpu.VMEM((2, SR, m, 512), BF),
         pltpu.VMEM((2, c.RM, 512), BF),
         pltpu.SemaphoreType.DMA((2, 2)),
-        pltpu.SemaphoreType.DMA((4,)),
+        pltpu.SemaphoreType.DMA((5,)),
         pltpu.SemaphoreType.DMA,
         *[pltpu.SemaphoreType.DMA((3, c.NK)) for _ in rows],
         pltpu.SemaphoreType.DMA((3, RING)),
@@ -60,15 +61,14 @@
         pltpu.SemaphoreType.DMA((3, SR)),
         pltpu.SemaphoreType.DMA((7,)),
         pltpu.SemaphoreType.DMA((2,)),
-        pltpu.SemaphoreType.REGULAR,
+        pltpu.SemaphoreType.REGULAR((2,)),
     ]
     return c
 
 
 def kernel(c, x, wg, wu, wd, y, *refs):
     S, m = c.S, c.M
-    land = [refs[3 * s : 3 * s + 3] for s in range(S)]
-    refs = refs[3 * S :]
+    land, refs = refs[:3], refs[3:]
     (xs, acc, kept, hid, gw, uw, dw, ss, lin, fin, out, yst, gsem, dsem, xsem), refs = refs[:15], refs[15:]
     agr, ags, rsr = refs[:S], refs[S], refs[S + 1 : 2 * S + 1]
     rss, lsem, ysem, free = refs[2 * S + 1 :]
@@ -161,7 +161,19 @@
         slot = lax.rem(u + 2 * SR, SR)
         to = [lambda: dev(zz + 1), lambda: dev(zz - 1), lambda: sib][way]()
         src = ss.at[slot, rows, :] if way == 2 else out.at[way, slot, rows, :]
-        return remote(src, land[s][way].at[u, rows, :], rss.at[way, slot], rsr[s].at[way, u], to)
+        return remote(src, landing(s, way, u, a, b), rss.at[way, slot], rsr[s].at[way, u], to)
+
+    def landing(s, way, u, a, b, h=None):
+        if s + 1 < S:
+            return land[way].at[u, pl.ds(a, b - a), :]
+        if way < 2:
+            cols = pl.ds(0, 512) if h is None else pl.ds(256 * h, 256)
+            return xs.at[u, pl.ds(way * m + a, b - a), cols]
+        row, col = lax.rem(u // 8, 2) * (c.KC // 2), lax.rem(u, 8) * 512
+        if h is not None:
+            col = col + 256 * h
+        cols = pl.ds(pl.multiple_of(col, 256), 512 if h is None else 256)
+        return gw.at[u // 16, pl.ds(pl.multiple_of(row + a, 16), b - a), cols]
 
     def rs_takes(s, zz, way):
         before = zz - 1 if way == 0 else zz + 1
@@ -175,31 +187,33 @@
         return b > a and (zz < 3 if way == 0 else zz > 0)
 
     def rs_unit(s, zz, part, tau):
-        return tau - A0 - LR * [zz, 3 - zz, max(zz, 3 - zz)][part]
+        return tau - A0[s] - LR[s] * [zz, 3 - zz, max(zz, 3 - zz)][part]
 
     def rs_loads(s, zz, part, u):
-        sb = land[s][2]
+        if s + 1 == S:
+            return []
+        sb = land[2]
         if part == 2:
             rows, n = pl.ds(c.off[s][zz], c.rows[s][zz]), pl.ds(0, c.rows[s][zz])
             cps = [(sb.at[u, rows, :], fin.at[2, n, :], 6)]
             for way in range(2):
                 if rs_takes(s, zz, way):
-                    cps.append((land[s][way].at[u, rows, :], fin.at[way, n, :], 4 + way))
+                    cps.append((land[way].at[u, rows, :], fin.at[way, n, :], 4 + way))
         else:
             a, b = rs_rows(s, zz, part)
             rows = pl.ds(a, b - a)
             cps = [(sb.at[u, rows, :], lin.at[2 + part, rows, :], 2 + part)]
             if rs_takes(s, zz, part):
-                cps.append((land[s][part].at[u, rows, :], lin.at[part, rows, :], part))
+                cps.append((land[part].at[u, rows, :], lin.at[part, rows, :], part))
         return [pltpu.make_async_copy(p, q, lsem.at[i]) for p, q, i in cps]
 
     def rs_parts(s, zz):
         return [p for p in range(3) if (c.rows[s][zz] > 0 if p == 2 else rs_sends(s, zz, p))]
 
     def rs_first(s, tau):
-        @pl.when(within(tau - A0, c.NU))
+        @pl.when(within(tau - A0[s], c.NU))
         def _():
-            rs_copy(s, 0, 2, tau - A0).wait_recv()
+            rs_copy(s, 0, 2, tau - A0[s]).wait_recv()
 
         def at(zz):
             for way in range(2):
@@ -226,12 +240,12 @@
                 u = rs_unit(s, zz, part, tau)
                 if part == 2:
                     a, b = c.off[s][zz], c.off[s][zz + 1]
-                    ins, to = (fin.at[2], fin.at[0], fin.at[1]), yst.at[lax.rem(u + 4, 2)]
-                    takes, lo, n = [rs_takes(s, zz, 0), rs_takes(s, zz, 1)], a, 2
+                    to, lo, n = yst.at[lax.rem(u + 4, 2)], a, 2
+                    takes = [2] + [w for w in range(2) if rs_takes(s, zz, w)]
                 else:
                     a, b = rs_rows(s, zz, part)
-                    ins, to = (lin.at[2 + part], lin.at[part]), out.at[part, lax.rem(u + 2 * SR, SR)]
-                    takes, lo, n = [rs_takes(s, zz, part)], 0, SR
+                    to, lo, n = out.at[part, lax.rem(u + 2 * SR, SR)], 0, SR
+                    takes = [2] + [part] * rs_takes(s, zz, part)
 
                 @pl.when(within(u - n, c.NU))
                 def _(u=u, part=part):
@@ -241,17 +255,21 @@
                         rs_copy(s, zz, part, u - SR).wait_send()
 
                 @pl.when(within(u, c.NU))
-                def _(u=u, part=part, a=a, b=b, ins=ins, to=to, takes=takes, lo=lo):
+                def _(u=u, part=part, a=a, b=b, to=to, takes=takes, lo=lo):
                     for cp in rs_loads(s, zz, part, u):
                         cp.wait()
-                    rows = pl.ds(a - lo, b - a)
                     for h in range(2):
                         cols = pl.ds(256 * h, 256)
-                        v = kept[2 * u + h, pl.ds(a, b - a), :] + ins[0][rows, cols].astype(F32)
-                        for i, take in enumerate(takes):
-                            if take:
-                                v = v + ins[1 + i][rows, cols].astype(F32)
-                        to[rows, cols] = v.astype(BF)
+                        v = kept[2 * u + h, pl.ds(a, b - a), :]
+                        for way in takes:
+                            if s + 1 == S:
+                                w = landing(s, way, u, a, b, h)[...]
+                            elif part == 2:
+                                w = fin[way, pl.ds(0, b - a), cols]
+                            else:
+                                w = lin[part + (2 if way == 2 else 0), pl.ds(a, b - a), cols]
+                            v = v + w.astype(F32)
+                        to[pl.ds(a - lo, b - a), cols] = v.astype(BF)
 
             for part in rs_parts(s, zz):
                 u = rs_unit(s, zz, part, tau)
@@ -296,28 +314,29 @@
 
         repeat(0, c.NK, chunk)
 
-    def activate():
+    def activate(s):
         def act(t):
             g, u = acc[t, :, pl.ds(0, 128)], acc[t, :, pl.ds(128, 128)]
             h = (g * jax.nn.sigmoid(g)) * u
             hid[:, pl.ds(pl.multiple_of(t * 128, 128), 128)] = h.astype(BF)
-            acc[t] = jnp.zeros((2 * m, 256), F32)
+            if s + 1 < S:
+                acc[t] = jnp.zeros((2 * m, 256), F32)
 
         repeat(0, c.NT, act)
 
     def down(s, before, after):
         def unit(u):
-            half = 2 * lax.rem(u, 2)
+            n = s * c.UN + 2 * u
             for h in range(2):
-                dcopy(0, half + h).wait()
-            for h in range(2):
+                dcopy(0, lax.rem(n + h, 5)).wait()
+            for h in range(3, 5):
                 if s + 1 < S:
-                    dcopy(lax.rem(2 * u + 2 + h, c.UN), 2 - half + h).start()
+                    dcopy(lax.rem(2 * u + h, c.UN), lax.rem(n + h, 5)).start()
                 else:
 
-                    @pl.when(u + 1 < c.NU)
+                    @pl.when(2 * u + h < c.UN)
                     def _(h=h):
-                        dcopy(2 * u + 2 + h, 2 - half + h).start()
+                        dcopy(2 * u + h, lax.rem(n + h, 5)).start()
 
             @pl.when(u >= SR)
             def _():
@@ -326,7 +345,7 @@
             before(u)
             slot = lax.rem(u, SR)
             for h in range(2):
-                v = jnp.dot(hid[...], dw[half + h], preferred_element_type=F32)
+                v = jnp.dot(hid[...], dw[lax.rem(n + h, 5)], preferred_element_type=F32)
                 kept[2 * u + h] = v[:m]
                 ss[slot, :, pl.ds(256 * h, 256)] = v[m:].astype(BF)
             rs_copy(s, 0, 2, u).start()
@@ -371,7 +390,7 @@
     own_start(0)
     for cp in gcopies(0, 0):
         cp.start()
-    for n in range(2):
+    for n in range(3):
         dcopy(n, n).start()
 
     def clear(t):
@@ -382,30 +401,42 @@
     na, nd = c.ag_lag[0] + 2, c.NU // 2
     repeat(0, 2, lambda t: ag_tick(0, t))
     repeat(0, c.NT, clear)
-    repeat(2, na, lambda t: ag_tick(0, t))
+    repeat(2, na - 1, lambda t: ag_tick(0, t))
     nothing = lambda t: None
-    gate_up(0, nothing, lambda k: ag_tick(0, k + na))
+
+    def after0(k):
+        pl.when(k == 0)(lambda: ag_tick(0, na - 1))
+        ag_tick(0, k + na)
+
+    gate_up(0, nothing, after0)
     repeat(c.NK + na, c.TA[0], lambda t: ag_tick(0, t))
-    tell(free)
+    tell(free.at[0])
     own_start(1)
-    activate()
+    activate(0)
 
     def before(u):
         @pl.when(u == 0)
         def _():
             own_wait(1)
-            hear(free)
-
-        pl.when(lax.rem(u, 2) == 0)(lambda: ag_tick(1, u // 2))
+            hear(free.at[0])
+
+        gathers = jnp.logical_and(lax.rem(u, 2) == 0, lax.rem(u, 8) != 6)
+        pl.when(gathers)(lambda: ag_tick(1, u // 8 * 3 + lax.rem(u, 8) // 2))
         pl.when(lax.rem(u, 2) == 1)(lambda: rs_first(0, u // 2))
 
     down(0, before, lambda u: pl.when(lax.rem(u, 2) == 1)(lambda: rs_second(0, u // 2)))
 
+    ng = 3 * c.NU // 8
+    assert ng > c.ag_lag[1] + 1
+    paced = 3 * c.NK // 4
+    rs_on = lambda k: jnp.logical_or(k >= paced, lax.rem(k, 3) != 2)
+    rs_at = lambda k: nd + jnp.where(k < paced, k - (k + 1) // 3, k - (paced + 1) // 3)
+
     def after(k):
-        rs_second(0, k + nd)
-        ag_tick(1, k + nd)
-
-    gate_up(1, lambda k: rs_first(0, k + nd), after)
+        pl.when(rs_on(k))(lambda: rs_second(0, rs_at(k)))
+        ag_tick(1, ng + k)
+
+    gate_up(1, lambda k: pl.when(rs_on(k))(lambda: rs_first(0, rs_at(k))), after)
 
     def both(s):
         def run(t):
@@ -413,15 +444,19 @@
             rs_second(s, t)
         return run
 
-    repeat(c.NK + nd, max(c.TA[1], c.NK + nd), lambda t: ag_tick(1, t))
-    repeat(c.NK + nd, max(c.TR[0], c.NK + nd), both(0))
-    activate()
-    down(1, lambda u: rs_first(1, u), lambda u: rs_second(1, u))
+    ag_done, rs_done = ng + c.NK, nd + c.NK - (paced + 1) // 3
+    assert ag_done >= c.NK + c.ag_lag[1]
+    repeat(ag_done, c.TA[1], lambda t: ag_tick(1, t))
+    repeat(rs_done, max(c.TR[0], rs_done), both(0))
+    tell(free.at[1])
+    activate(1)
+
+    down(1, lambda u: pl.when(u == 0)(lambda: hear(free.at[1])), both(1))
     repeat(c.NU, c.TR[1], both(1))
 
 
 def block(c, x, wg, wu, wd):
-    lands = [jax.ShapeDtypeStruct((c.NU, c.M, 512), BF) for _ in range(3 * c.S)]
+    lands = [jax.ShapeDtypeStruct((c.NU, c.M, 512), BF) for _ in range(3)]
     hbm = pl.BlockSpec(memory_space=pltpu.HBM)
     outs = pl.pallas_call(
         functools.partial(kernel, c),

time: 367 us -> 348 us (0.948)
  Pallas kernels: 362 us -> 344 us
    pallas_call x1, Pallas kernels: 362 us -> 344 us  [block(): pl.pallas_call(functools.partial(kernel, c), out_shape=[jax.ShapeDtypeStr...]
where the time goes in v2:
time: 348 us
  Pallas kernels  344 us (99%)
    pallas_call x1, Pallas kernels, block(): pl.pallas_call(functools.partial(kernel, c), out_shape=[jax.ShapeDtypeStr...  344 us

profile of v2, /device:TPU:0, one launch (start us, length us, event | category | flops | bytes accessed | tf_op | source)
XLA Modules:
  0.0 347.6 jit_solution(4539751283699222704)
XLA Ops:
  0.0 344.3 %mlp.1 = (bf16[96,12288]{1,0:T(8,128)(2,1)}, bf16[24,192,512]{2,1,0:T(8,128)(2,1)}, bf16[24,192,512]{2,1,0:T(8,128)(2,1)}, bf16[24,192,512]{2,1,0:T(8,128)(2,1)}) custom-call(bf16[96,12288]{1,0:T(8,128)(2,1)} %x.1, bf16[12288,4224]{1,0:T(8,128)(2,1)} %wg.1, bf16[12288,4224]{1,0:T(8,128)(2,1)} %wu.1, bf16[4224,12288]{1,0:T(8,128)(2,1)} %wd.1), custom_call_target="tpu_custom_call" | custom-call | tf_op jit(solution)/shard_map/mlp/pallas_call | solution.py:461
  344.4 3.2 copy.6

commit v3 on v2

--- a/solution.py
+++ b/solution.py
@@ -55,9 +55,8 @@
         pltpu.SemaphoreType.DMA((2, 2)),
         pltpu.SemaphoreType.DMA((5,)),
         pltpu.SemaphoreType.DMA,
-        *[pltpu.SemaphoreType.DMA((3, c.NK)) for _ in rows],
+        *[pltpu.SemaphoreType.DMA((3, max(c.NK, c.NU))) for _ in rows],
         pltpu.SemaphoreType.DMA((3, RING)),
-        *[pltpu.SemaphoreType.DMA((3, c.NU)) for _ in rows],
         pltpu.SemaphoreType.DMA((3, SR)),
         pltpu.SemaphoreType.DMA((7,)),
         pltpu.SemaphoreType.DMA((2,)),
@@ -70,8 +69,9 @@
     S, m = c.S, c.M
     land, refs = refs[:3], refs[3:]
     (xs, acc, kept, hid, gw, uw, dw, ss, lin, fin, out, yst, gsem, dsem, xsem), refs = refs[:15], refs[15:]
-    agr, ags, rsr = refs[:S], refs[S], refs[S + 1 : 2 * S + 1]
-    rss, lsem, ysem, free = refs[2 * S + 1 :]
+    agr, ags = refs[:S], refs[S]
+    rsr = agr
+    rss, lsem, ysem, free = refs[S + 1 :]
 
     tp = lax.axis_index("tp")
     z, core = tp // 2, lax.rem(tp, 2)
@@ -290,39 +290,37 @@
         return pltpu.make_async_copy(yst.at[slot, pl.ds(0, r), :], y.at[at], ysem.at[slot])
 
     def gate_up(s, before, after):
-        def chunk(k):
+        def chunk(k, last=False):
             slot = lax.rem(k, 2)
             for cp in gcopies(k, slot):
                 cp.wait()
             ag_copy(s, 0, 2, k).wait_recv()
             if s + 1 < S:
                 for cp in gcopies(lax.rem(k + 1, c.NK), 1 - slot):
-                    cp.start()
+                    cp.start(priority=1)
             else:
 
                 @pl.when(k + 1 < c.NK)
                 def _():
                     for cp in gcopies(k + 1, 1 - slot):
-                        cp.start()
+                        cp.start(priority=1)
 
             before(k)
             for t in range(c.NT):
                 cols = pl.ds(t * 128, 128)
                 w = jnp.concatenate([gw[slot, :, cols], uw[slot, :, cols]], axis=1)
-                acc[t] += jnp.dot(xs[k], w, preferred_element_type=F32)
+                v = acc[t] + jnp.dot(xs[k], w, preferred_element_type=F32)
+                if not last:
+                    acc[t] = v
+                    continue
+                g, u = v[:, :128], v[:, 128:]
+                hid[:, cols] = ((g * jax.nn.sigmoid(g)) * u).astype(BF)
+                if s + 1 < S:
+                    acc[t] = jnp.zeros((2 * m, 256), F32)
             after(k)
 
-        repeat(0, c.NK, chunk)
-
-    def activate(s):
-        def act(t):
-            g, u = acc[t, :, pl.ds(0, 128)], acc[t, :, pl.ds(128, 128)]
-            h = (g * jax.nn.sigmoid(g)) * u
-            hid[:, pl.ds(pl.multiple_of(t * 128, 128), 128)] = h.astype(BF)
-            if s + 1 < S:
-                acc[t] = jnp.zeros((2 * m, 256), F32)
-
-        repeat(0, c.NT, act)
+        repeat(0, c.NK - 1, chunk)
+        chunk(jnp.int32(c.NK - 1), True)
 
     def down(s, before, after):
         def unit(u):
@@ -331,12 +329,12 @@
                 dcopy(0, lax.rem(n + h, 5)).wait()
             for h in range(3, 5):
                 if s + 1 < S:
-                    dcopy(lax.rem(2 * u + h, c.UN), lax.rem(n + h, 5)).start()
+                    dcopy(lax.rem(2 * u + h, c.UN), lax.rem(n + h, 5)).start(priority=1)
                 else:
 
                     @pl.when(2 * u + h < c.UN)
                     def _(h=h):
-                        dcopy(2 * u + h, lax.rem(n + h, 5)).start()
+                        dcopy(2 * u + h, lax.rem(n + h, 5)).start(priority=1)
 
             @pl.when(u >= SR)
             def _():
@@ -412,7 +410,6 @@
     repeat(c.NK + na, c.TA[0], lambda t: ag_tick(0, t))
     tell(free.at[0])
     own_start(1)
-    activate(0)
 
     def before(u):
         @pl.when(u == 0)
@@ -433,8 +430,8 @@
     rs_at = lambda k: nd + jnp.where(k < paced, k - (k + 1) // 3, k - (paced + 1) // 3)
 
     def after(k):
+        ag_tick(1, ng + k)
         pl.when(rs_on(k))(lambda: rs_second(0, rs_at(k)))
-        ag_tick(1, ng + k)
 
     gate_up(1, lambda k: pl.when(rs_on(k))(lambda: rs_first(0, rs_at(k))), after)
 
@@ -449,7 +446,6 @@
     repeat(ag_done, c.TA[1], lambda t: ag_tick(1, t))
     repeat(rs_done, max(c.TR[0], rs_done), both(0))
     tell(free.at[1])
-    activate(1)
 
     down(1, lambda u: pl.when(u == 0)(lambda: hear(free.at[1])), both(1))
     repeat(c.NU, c.TR[1], both(1))

time: 348 us -> 344 us (0.989)
  no operation moved by 1% of the time
where the time goes in v3:
time: 344 us
  Pallas kernels  341 us (99%)
    pallas_call x1, Pallas kernels, block(): pl.pallas_call(functools.partial(kernel, c), out_shape=[jax.ShapeDtypeStr...  341 us

profile of v3, /device:TPU:0, one launch (start us, length us, event | category | flops | bytes accessed | tf_op | source)
XLA Modules:
  0.0 344.2 jit_solution(4326637867951455134)
XLA Ops:
  0.0 341.0 %mlp.1 = (bf16[96,12288]{1,0:T(8,128)(2,1)}, bf16[24,192,512]{2,1,0:T(8,128)(2,1)}, bf16[24,192,512]{2,1,0:T(8,128)(2,1)}, bf16[24,192,512]{2,1,0:T(8,128)(2,1)}) custom-call(bf16[96,12288]{1,0:T(8,128)(2,1)} %x.1, bf16[12288,4224]{1,0:T(8,128)(2,1)} %wg.1, bf16[12288,4224]{1,0:T(8,128)(2,1)} %wu.1, bf16[4224,12288]{1,0:T(8,128)(2,1)} %wd.1), custom_call_target="tpu_custom_call" | custom-call | tf_op jit(solution)/shard_map/mlp/pallas_call | solution.py:457
  341.0 3.2 copy.6
